TPU v7x, 32 devices: a whole 2x2x4 slice. The times are simulated.
32 devices in a mesh: dp: 8 (over y, x, core), group: 4 (over z).
Axes of the slice: x: 2, y: 2, z: 4, core: 2. Of those that a mesh axis runs over, the one named last changes fastest.
Arguments:
- images: bfloat16 [4096, 512], P(('dp', 'group')), may hold values from -1 to 1
- texts: bfloat16 [4096, 512], P(('dp', 'group')), may hold values from -1 to 1
- log_scale: float32 [], replicated, may hold values from 2 to 2.7
Outputs:
- grad_images: bfloat16 [4096, 512], P(('dp', 'group'))
- grad_texts: bfloat16 [4096, 512], P(('dp', 'group'))
- loss: float32 [], replicated
- grad_scale: float32 [], replicated
All inputs are finite; a program needn't handle non-finite values.
Results may differ from a plain program's by a relative error of at most 0.0013.
The roundings to bfloat16 on the way count: a program that leaves them out, or rounds other values in their place, can miss the bound.
Values may be sent and summed in bfloat16 or wider, within the bound.
A program may use at most 128 MiB of HBM per device.

v0:
```python
import jax
import jax.numpy as jnp
from jax import lax
from jax.sharding import PartitionSpec as P


def body(images, texts, log_scale):
    row_count = images.shape[0]
    device_count = lax.axis_size(("dp", "group"))
    pair_total = row_count * device_count
    within = lax.all_gather(texts, "group", axis=0, tiled=True)
    texts_whole = lax.all_gather(within, "dp", axis=0, tiled=True)
    images_whole = lax.all_gather(images, ("dp", "group"), axis=0, tiled=True)
    logit_scale = jnp.exp(log_scale)
    first_pair = lax.axis_index(("dp", "group")) * row_count
    contract_last = (((1,), (1,)), ((), ()))
    contract_first = (((0,), (0,)), ((), ()))
    row_logits = logit_scale * lax.dot_general(
        images, texts_whole, contract_last, preferred_element_type=jnp.float32
    )
    row_top = jnp.max(row_logits, axis=1)
    row_lse = row_top + jnp.log(jnp.sum(jnp.exp(row_logits - row_top[:, None]), axis=1))
    paired = jnp.diagonal(lax.dynamic_slice_in_dim(row_logits, first_pair, row_count, 1))
    part_top = jnp.max(row_logits, axis=0)
    part_sum = jnp.sum(jnp.exp(row_logits - part_top[None, :]), axis=0)
    got_top, got_sum = (
        lax.all_to_all(
            part_top.reshape(device_count, row_count),
            ("dp", "group"),
            split_axis=0,
            concat_axis=0,
            tiled=True,
        ),
        lax.all_to_all(
            part_sum.reshape(device_count, row_count),
            ("dp", "group"),
            split_axis=0,
            concat_axis=0,
            tiled=True,
        ),
    )
    col_top = jnp.max(got_top, axis=0)
    col_lse = col_top + jnp.log(jnp.sum(got_sum * jnp.exp(got_top - col_top[None, :]), axis=0))
    row_whole, col_whole = (
        lax.all_gather(row_lse, ("dp", "group"), axis=0, tiled=True),
        lax.all_gather(col_lse, ("dp", "group"), axis=0, tiled=True),
    )
    own_pairs = (
        jnp.arange(pair_total)[None, :] == (first_pair + jnp.arange(row_count))[:, None]
    ).astype(jnp.float32)
    row_grad = (
        0.5 * (jnp.exp(row_logits - row_lse[:, None]) + jnp.exp(row_logits - col_whole[None, :]))
        - own_pairs
    )
    scale_part = jnp.sum(row_grad * row_logits)
    row_weights = row_grad.astype(jnp.bfloat16)
    grad_images = (
        logit_scale * jnp.dot(row_weights, texts_whole, preferred_element_type=jnp.float32)
    ).astype(jnp.bfloat16)
    col_logits = logit_scale * lax.dot_general(
        images_whole, texts, contract_last, preferred_element_type=jnp.float32
    )
    col_grad = (
        0.5 * (jnp.exp(col_logits - row_whole[:, None]) + jnp.exp(col_logits - col_lse[None, :]))
        - own_pairs.T
    )
    text_sum = logit_scale * lax.dot_general(
        col_grad.astype(jnp.bfloat16),
        images_whole,
        contract_first,
        preferred_element_type=jnp.float32,
    )
    grad_texts = text_sum.astype(jnp.bfloat16)
    loss_part = jnp.sum(row_lse) + jnp.sum(col_lse) - 2.0 * jnp.sum(paired)
    loss_total, scale_total = lax.psum((loss_part, scale_part), ("dp", "group"))
    return (grad_images, grad_texts, loss_total / (2.0 * pair_total), scale_total / pair_total)


def solution(mesh):
    in_specs = (P(("dp", "group"), None), P(("dp", "group"), None), P())
    out_specs = (P(("dp", "group"), None), P(("dp", "group"), None), P(), P())
    return jax.shard_map(body, mesh=mesh, in_specs=in_specs, out_specs=out_specs, check_vma=False)
```

profile of v0, /device:TPU:0, one launch (start us, length us, event | category | flops | bytes accessed | tf_op | source)
XLA Modules:
  0.0 281.2 jit_solution(1704532022172781684)
XLA Ops:
  7.2 0.0 all-gather.5.cloned.1.call-start
  7.2 19.3 %all_gather.15 = bf16[512,512]{1,0:T(8,128)(2,1)} all-gather(bf16[128,512]{1,0:T(8,128)(2,1)} %param.4), channel_id=1, replica_groups=mesh['dp'=8,'group'=4] {'group'}, dimensions={0}, use_global_device_ids=true | all-gather | bytes 655360 | tf_op jit(solution)/shard_map/all_gather | solution.py:11
  26.5 0.0 all-gather.5.cloned.1.call-update
  26.6 0.0 all-gather.7.cloned.1.call-start
  26.6 0.7 all-gather.7.cloned.1.call-update
  28.0 35.0 %all-gather.5.cloned.1.call-done = bf16[4096,512]{1,0:T(8,128)(2,1)} async-done(((bf16[512,512]{1,0:T(8,128)(2,1)}), bf16[4096,512]{1,0:T(8,128)(2,1)}) %all-gather.5.cloned.1.call-update) | async-done | bytes 4194320 | tf_op jit(solution)/shard_map/all_gather | solution.py:12
  63.1 4.4 %fusion.10 = (f32[128]{0:T(128)S(1)}, f32[4096]{0:T(1024)}, f32[128,4096]{1,0:T(8,128)S(1)}) fusion(bf16[128,512]{1,0:T(8,128)(2,1)} %param.3, bf16[4096,512]{1,0:T(8,128)(2,1)} %all-gather.5.cloned.1.call-done, f32[]{:T(128)S(6)} %exp.24), kind=kOutput, calls=%fused_computation.27 | convolution fusion | flops 538439552 | bytes 6439428 | tf_op jit(solution)/shard_map/dot_general | solution.py:18
  67.5 4.6 %all-to-all-start = ((f32[32,1,128]{2,1,0:T(1,128)}), f32[32,1,128]{2,1,0:T(1,128)S(1)}, u32[]{:S(2)}, u32[]{:S(2)}) async-start(f32[32,1,128]{2,1,0:T(1,128)} %bitcast), calls=%async_computation | async-start | bytes 32768 | tf_op jit(solution)/shard_map/all_to_all | solution.py:27
  72.1 2.0 exponential_reduce_fusion.1
  74.2 0.6 fusion.12
  74.8 4.5 %all-to-all-done = f32[32,1,128]{2,1,0:T(1,128)S(1)} async-done(((f32[32,1,128]{2,1,0:T(1,128)}), f32[32,1,128]{2,1,0:T(1,128)S(1)}, u32[]{:S(2)}, u32[]{:S(2)}) %all-to-all-start) | async-done | bytes 16416 | tf_op jit(solution)/shard_map/all_to_all | solution.py:27
  79.2 2.5 all-to-all-start.1
  81.8 1.2 gather_fusion
  83.1 0.6 reduce_sum.68
  84.3 0.1 reduce_max.29
  84.4 4.6 %all-to-all-done.1 = f32[32,1,128]{2,1,0:T(1,128)S(1)} async-done(((f32[32,1,128]{2,1,0:T(1,128)}), f32[32,1,128]{2,1,0:T(1,128)S(1)}, u32[]{:S(2)}, u32[]{:S(2)}) %all-to-all-start.1) | async-done | bytes 16416 | tf_op jit(solution)/shard_map/all_to_all | solution.py:34
  89.0 0.6 fusion.11
  90.9 64.1 %all-gather = f32[32,1,128]{2,1,0:T(1,128)S(1)} all-gather(f32[1,1,128]{2,1,0:T(1,128)S(1)} %bitcast.22), channel_id=1, replica_groups=mesh['dp'=8,'group'=4] {'dp','group'}, dimensions={0}, use_global_device_ids=true | all-gather | bytes 16896 | tf_op jit(solution)/shard_map/all_gather | solution.py:46
  155.0 1.5 multiply_reduce_fusion
  156.5 65.1 %all-gather.1 = f32[32,1,128]{2,1,0:T(1,128)S(1)} all-gather(f32[1,1,128]{2,1,0:T(1,128)S(1)} %bitcast.21), channel_id=1, replica_groups=mesh['dp'=8,'group'=4] {'dp','group'}, dimensions={0}, use_global_device_ids=true | all-gather | bytes 16896 | tf_op jit(solution)/shard_map/all_gather | solution.py:45
  221.6 38.4 %all-reduce = (f32[]{:T(128)}, f32[]{:T(128)}) all-reduce(f32[]{:T(128)S(6)} %sub.81, f32[]{:T(128)} %multiply_reduce_fusion), channel_id=1, replica_groups=mesh['dp'=8,'group'=4] {'dp','group'}, use_global_device_ids=true, to_apply=%region_9.10 | all-reduce | flops 2 | bytes 16 | tf_op jit(solution)/shard_map/psum | solution.py:75
  261.4 0.0 copy-start
  261.4 4.0 %fusion.1 = bf16[128,512]{1,0:T(8,128)(2,1)} fusion(bf16[4096,512]{1,0:T(8,128)(2,1)} %all-gather.5.cloned.1.call-done, f32[128,4096]{1,0:T(8,128)S(1)} %get-tuple-element.14, s32[128]{0:T(128)S(1)} %iota_add_fusion, f32[4096]{0:T(1024)S(1)} %bitcast.18, f32[128]{0:T(128)S(1)} %get-tuple-element.13, f32[]{:T(128)S(6)} %exp.24), kind=kOutput, calls=%fused_computation.13 | convolution fusion | flops 541196288 | bytes 6439940 | tf_op jit(solution)/shard_map/dot_general | solution.py:58
  265.4 0.0 all-gather.7.cloned.1.call-done
  265.4 0.0 copy-done
  265.4 6.7 %fusion.2 = bf16[128,512]{1,0:T(8,128)(2,1)} fusion(bf16[4096,512]{1,0:T(8,128)(2,1)} %all-gather.7.cloned.1.call-done, bf16[128,512]{1,0:T(8,128)(2,1)S(1)} %copy-done, s32[128]{0:T(128)S(1)} %iota_add_fusion, f32[128]{0:T(128)S(1)} %get-tuple-element.11, f32[4096]{0:T(1024)S(1)} %bitcast.20, f32[]{:T(128)S(6)} %exp.24), kind=kOutput, calls=%fused_computation.14 | convolution fusion | flops 1078591488 | bytes 4473860 | tf_op jit(solution)/shard_map/dot_general | solution.py:67
  (4 shorter events, 0.1 us)
Async XLA Ops:
  7.2 55.9 %all-gather.5.cloned.1.call-start = ((), (), s32[]{:S(2)}) async-start(), calls=%async_computation.2 | async-start | bytes 4718592 | tf_op jit(solution)/shard_map/all_gather | solution.py:12
  26.6 238.8 %all-gather.7.cloned.1.call-start = ((), (), s32[]{:S(2)}) async-start(), calls=%async_computation.3 | async-start | bytes 4325376 | tf_op jit(solution)/shard_map/all_gather | solution.py:13
  67.5 11.7 %all-to-all-start = ((f32[32,1,128]{2,1,0:T(1,128)}), f32[32,1,128]{2,1,0:T(1,128)S(1)}, u32[]{:S(2)}, u32[]{:S(2)}) async-start(f32[32,1,128]{2,1,0:T(1,128)} %bitcast), calls=%async_computation | async-start | bytes 32768 | tf_op jit(solution)/shard_map/all_to_all | solution.py:27
  79.2 9.7 %all-to-all-start.1 = ((f32[32,1,128]{2,1,0:T(1,128)}), f32[32,1,128]{2,1,0:T(1,128)S(1)}, u32[]{:S(2)}, u32[]{:S(2)}) async-start(f32[32,1,128]{2,1,0:T(1,128)} %bitcast.1), calls=%async_computation.1 | async-start | bytes 32768 | tf_op jit(solution)/shard_map/all_to_all | solution.py:34
  261.4 4.0 %copy-start = (bf16[128,512]{1,0:T(8,128)(2,1)S(1)}, bf16[128,512]{1,0:T(8,128)(2,1)}, u32[]{:S(2)}) copy-start(bf16[128,512]{1,0:T(8,128)(2,1)} %param.4) | copy-start | bytes 393220
Sparse Core Ops, SparseCore 0:
  26.7 36.3 all-gather.4
  66.1 61.6 all-gather.6
where the time goes:
time: 282 us; the launch traced here: 281 us
  blocking collectives  187 us (66%)
  waiting for transfers between devices  44.8 us (16%)
  between operations  20.3 us (7%)
  matrix products  15.1 us (5%)
  starting transfers between devices  7.21 us (3%)
  other arithmetic  5.48 us (2%)
    all_gather x1, blocking collectives, body(): lax.all_gather(row_lse, ('dp', 'group'), axis=0, tiled=True)  65.1 us
    all_gather x1, blocking collectives, body(): lax.all_gather(col_lse, ('dp', 'group'), axis=0, tiled=True)  64.1 us
    psum x1, blocking collectives, body(): loss_total, scale_total = lax.psum((loss_part, scale_part), ('dp', 'group'))  38.4 us
    all_gather x1, waiting for transfers between devices, body(): texts_whole = lax.all_gather(within, 'dp', axis=0, tiled=True)  35 us
    all_gather x1, blocking collectives, body(): within = lax.all_gather(texts, 'group', axis=0, tiled=True)  19.3 us
    dot_general x1, matrix products, body(): lax.dot_general(col_grad.astype(jnp.bfloat16), images_whole, contract_fir...  6.7 us
  transfers between devices with their start and end apart: 4, of which 3 were waited for; matrix products, arithmetic and copies ran while one was open for 5% of the time, Pallas kernels for 0%

commit v1 on v0

--- a/solution.py
+++ b/solution.py
@@ -72,7 +72,9 @@
     )
     grad_texts = text_sum.astype(jnp.bfloat16)
     loss_part = jnp.sum(row_lse) + jnp.sum(col_lse) - 2.0 * jnp.sum(paired)
-    loss_total, scale_total = lax.psum((loss_part, scale_part), ("dp", "group"))
+    loss_total, scale_total = lax.psum(
+        lax.psum((loss_part, scale_part), axis_name="group"), axis_name="dp"
+    )
     return (grad_images, grad_texts, loss_total / (2.0 * pair_total), scale_total / pair_total)
 
 

time: 282 us -> 265 us (0.940)
  blocking collectives: 187 us -> 170 us
    psum x1 -> x2, blocking collectives: 38.4 us -> 22 us  [the longest x1 12.4 us: body(): lax.psum(lax.psum((loss_part, scale_part), axis_name='group'), axis_name=...]
  transfers between devices with their start and end apart: 4 -> 4, of which waited for: 3 -> 3; matrix products, arithmetic and copies ran while one was open for 5% -> 6% of each run, Pallas kernels for 0% -> 0%
where the time goes in v1:
time: 265 us
  blocking collectives  170 us (64%)
  waiting for transfers between devices  44.8 us (17%)
  between operations  20.3 us (8%)
  matrix products  15.1 us (6%)
  starting transfers between devices  7.21 us (3%)
  other arithmetic  5.48 us (2%)
    all_gather x1, blocking collectives, body(): lax.all_gather(row_lse, ('dp', 'group'), axis=0, tiled=True)  65.1 us
    all_gather x1, blocking collectives, body(): lax.all_gather(col_lse, ('dp', 'group'), axis=0, tiled=True)  64.1 us
    all_gather x1, waiting for transfers between devices, body(): texts_whole = lax.all_gather(within, 'dp', axis=0, tiled=True)  35 us
    all_gather x1, blocking collectives, body(): within = lax.all_gather(texts, 'group', axis=0, tiled=True)  19.3 us
    psum x1, blocking collectives, body(): lax.psum(lax.psum((loss_part, scale_part), axis_name='group'), axis_name=...  12.4 us
    psum x1, blocking collectives, body(): lax.psum((loss_part, scale_part), axis_name='group')  9.57 us
    dot_general x1, matrix products, body(): lax.dot_general(col_grad.astype(jnp.bfloat16), images_whole, contract_fir...  6.7 us
  transfers between devices with their start and end apart: 4, of which 3 were waited for; matrix products, arithmetic and copies ran while one was open for 6% of the time, Pallas kernels for 0%

profile of v1, /device:TPU:0, one launch (start us, length us, event | category | flops | bytes accessed | tf_op | source)
XLA Modules:
  0.0 264.7 jit_solution(10815658415297479351)
XLA Ops:
  7.2 0.0 all-gather.5.cloned.1.call-start
  7.2 19.3 %all_gather.15 = bf16[512,512]{1,0:T(8,128)(2,1)} all-gather(bf16[128,512]{1,0:T(8,128)(2,1)} %param.4), channel_id=1, replica_groups=mesh['dp'=8,'group'=4] {'group'}, dimensions={0}, use_global_device_ids=true | all-gather | bytes 655360 | tf_op jit(solution)/shard_map/all_gather | solution.py:11
  26.5 0.0 all-gather.5.cloned.1.call-update
  26.6 0.0 all-gather.7.cloned.1.call-start
  26.6 0.7 all-gather.7.cloned.1.call-update
  28.0 35.0 %all-gather.5.cloned.1.call-done = bf16[4096,512]{1,0:T(8,128)(2,1)} async-done(((bf16[512,512]{1,0:T(8,128)(2,1)}), bf16[4096,512]{1,0:T(8,128)(2,1)}) %all-gather.5.cloned.1.call-update) | async-done | bytes 4194320 | tf_op jit(solution)/shard_map/all_gather | solution.py:12
  63.1 4.4 %fusion.10 = (f32[128]{0:T(128)S(1)}, f32[4096]{0:T(1024)}, f32[128,4096]{1,0:T(8,128)S(1)}) fusion(bf16[128,512]{1,0:T(8,128)(2,1)} %param.3, bf16[4096,512]{1,0:T(8,128)(2,1)} %all-gather.5.cloned.1.call-done, f32[]{:T(128)S(6)} %exp.24), kind=kOutput, calls=%fused_computation.27 | convolution fusion | flops 538439552 | bytes 6439428 | tf_op jit(solution)/shard_map/dot_general | solution.py:18
  67.5 4.6 %all-to-all-start = ((f32[32,1,128]{2,1,0:T(1,128)}), f32[32,1,128]{2,1,0:T(1,128)S(1)}, u32[]{:S(2)}, u32[]{:S(2)}) async-start(f32[32,1,128]{2,1,0:T(1,128)} %bitcast), calls=%async_computation | async-start | bytes 32768 | tf_op jit(solution)/shard_map/all_to_all | solution.py:27
  72.1 2.0 exponential_reduce_fusion.1
  74.2 0.6 fusion.12
  74.8 4.5 %all-to-all-done = f32[32,1,128]{2,1,0:T(1,128)S(1)} async-done(((f32[32,1,128]{2,1,0:T(1,128)}), f32[32,1,128]{2,1,0:T(1,128)S(1)}, u32[]{:S(2)}, u32[]{:S(2)}) %all-to-all-start) | async-done | bytes 16416 | tf_op jit(solution)/shard_map/all_to_all | solution.py:27
  79.2 2.5 all-to-all-start.1
  81.8 1.2 gather_fusion
  83.1 0.6 reduce_sum.68
  84.3 0.1 reduce_max.29
  84.4 4.6 %all-to-all-done.1 = f32[32,1,128]{2,1,0:T(1,128)S(1)} async-done(((f32[32,1,128]{2,1,0:T(1,128)}), f32[32,1,128]{2,1,0:T(1,128)S(1)}, u32[]{:S(2)}, u32[]{:S(2)}) %all-to-all-start.1) | async-done | bytes 16416 | tf_op jit(solution)/shard_map/all_to_all | solution.py:34
  89.0 0.6 fusion.11
  90.9 64.1 %all-gather = f32[32,1,128]{2,1,0:T(1,128)S(1)} all-gather(f32[1,1,128]{2,1,0:T(1,128)S(1)} %bitcast.22), channel_id=1, replica_groups=mesh['dp'=8,'group'=4] {'dp','group'}, dimensions={0}, use_global_device_ids=true | all-gather | bytes 16896 | tf_op jit(solution)/shard_map/all_gather | solution.py:46
  155.0 1.5 multiply_reduce_fusion
  156.5 65.1 %all-gather.1 = f32[32,1,128]{2,1,0:T(1,128)S(1)} all-gather(f32[1,1,128]{2,1,0:T(1,128)S(1)} %bitcast.21), channel_id=1, replica_groups=mesh['dp'=8,'group'=4] {'dp','group'}, dimensions={0}, use_global_device_ids=true | all-gather | bytes 16896 | tf_op jit(solution)/shard_map/all_gather | solution.py:45
  221.6 9.6 %all-reduce.1 = (f32[]{:T(128)}, f32[]{:T(128)}) all-reduce(f32[]{:T(128)S(6)} %sub.81, f32[]{:T(128)} %multiply_reduce_fusion), channel_id=1, replica_groups=mesh['dp'=8,'group'=4] {'group'}, use_global_device_ids=true, to_apply=%region_9.10 | all-reduce | flops 2 | bytes 16 | tf_op jit(solution)/shard_map/psum | solution.py:76
  231.2 12.4 %all-reduce = (f32[]{:T(128)}, f32[]{:T(128)}) all-reduce(f32[]{:T(128)} %get-tuple-element.10, f32[]{:T(128)} %get-tuple-element.11), channel_id=1, replica_groups=mesh['dp'=8,'group'=4] {'dp'}, use_global_device_ids=true, to_apply=%region_10.11 | all-reduce | flops 2 | bytes 16 | tf_op jit(solution)/shard_map/psum | solution.py:75
  244.9 0.0 copy-start
  244.9 4.0 %fusion.1 = bf16[128,512]{1,0:T(8,128)(2,1)} fusion(bf16[4096,512]{1,0:T(8,128)(2,1)} %all-gather.5.cloned.1.call-done, f32[128,4096]{1,0:T(8,128)S(1)} %get-tuple-element.16, s32[128]{0:T(128)S(1)} %iota_add_fusion, f32[4096]{0:T(1024)S(1)} %bitcast.18, f32[128]{0:T(128)S(1)} %get-tuple-element.15, f32[]{:T(128)S(6)} %exp.24), kind=kOutput, calls=%fused_computation.13 | convolution fusion | flops 541196288 | bytes 6439940 | tf_op jit(solution)/shard_map/dot_general | solution.py:58
  248.9 0.0 all-gather.7.cloned.1.call-done
  248.9 0.0 copy-done
  248.9 6.7 %fusion.2 = bf16[128,512]{1,0:T(8,128)(2,1)} fusion(bf16[4096,512]{1,0:T(8,128)(2,1)} %all-gather.7.cloned.1.call-done, bf16[128,512]{1,0:T(8,128)(2,1)S(1)} %copy-done, s32[128]{0:T(128)S(1)} %iota_add_fusion, f32[128]{0:T(128)S(1)} %get-tuple-element.13, f32[4096]{0:T(1024)S(1)} %bitcast.20, f32[]{:T(128)S(6)} %exp.24), kind=kOutput, calls=%fused_computation.14 | convolution fusion | flops 1078591488 | bytes 4473860 | tf_op jit(solution)/shard_map/dot_general | solution.py:67
  (4 shorter events, 0.1 us)
Async XLA Ops:
  7.2 55.9 %all-gather.5.cloned.1.call-start = ((), (), s32[]{:S(2)}) async-start(), calls=%async_computation.2 | async-start | bytes 4718592 | tf_op jit(solution)/shard_map/all_gather | solution.py:12
  26.6 222.3 %all-gather.7.cloned.1.call-start = ((), (), s32[]{:S(2)}) async-start(), calls=%async_computation.3 | async-start | bytes 4325376 | tf_op jit(solution)/shard_map/all_gather | solution.py:13
  67.5 11.7 %all-to-all-start = ((f32[32,1,128]{2,1,0:T(1,128)}), f32[32,1,128]{2,1,0:T(1,128)S(1)}, u32[]{:S(2)}, u32[]{:S(2)}) async-start(f32[32,1,128]{2,1,0:T(1,128)} %bitcast), calls=%async_computation | async-start | bytes 32768 | tf_op jit(solution)/shard_map/all_to_all | solution.py:27
  79.2 9.7 %all-to-all-start.1 = ((f32[32,1,128]{2,1,0:T(1,128)}), f32[32,1,128]{2,1,0:T(1,128)S(1)}, u32[]{:S(2)}, u32[]{:S(2)}) async-start(f32[32,1,128]{2,1,0:T(1,128)} %bitcast.1), calls=%async_computation.1 | async-start | bytes 32768 | tf_op jit(solution)/shard_map/all_to_all | solution.py:34
  244.9 4.0 %copy-start = (bf16[128,512]{1,0:T(8,128)(2,1)S(1)}, bf16[128,512]{1,0:T(8,128)(2,1)}, u32[]{:S(2)}) copy-start(bf16[128,512]{1,0:T(8,128)(2,1)} %param.4) | copy-start | bytes 393220
Sparse Core Ops, SparseCore 0:
  26.7 36.3 all-gather.4
  66.1 61.6 all-gather.6
